TPU v7x, 32 devices: a whole 2x2x4 slice. The times are simulated.
32 devices in a mesh: node: 8 (over z, x), feat: 4 (over y, core).
Axes of the slice: x: 2, y: 2, z: 4, core: 2. Of those that a mesh axis runs over, the one named last changes fastest.
Arguments:
- features: bfloat16 [100, 8192], P('feat', 'node'), may hold values from -6 to 6
- edges_one: int32 [1024, 8192], P(None, 'node'), may hold values from 0 to 1, as said below
- w1_self: bfloat16 [100, 256], P('feat'), may hold values from -0.625 to 0.625
- w1_nbr: bfloat16 [100, 256], P('feat'), may hold values from -1.25 to 1.25
- need_blocks: int32 [8, 4], P('node'), may hold values from 0 to 7, as said below
- live_slots: int32 [8, 4], P('node'), may hold values from 0 to 1, as said below
- edges_two: int32 [4096, 8192], P(None, 'node'), may hold values from 0 to 1, as said below
- w2_self: bfloat16 [256, 47], P('feat'), may hold values from -0.375 to 0.375
- w2_nbr: bfloat16 [256, 47], P('feat'), may hold values from -0.5 to 0.5
- labels: int32 [8192], P('node'), may hold values from 0 to 46
Outputs:
- node_loss: float32 [8192], P('node')
- mean_loss: float32 [], replicated
Inputs may be any that keep to these rules, and one draw needn't show every extreme that they name: `need_blocks`: row b holds 4 different blocks; its first entry is b, its second is b plus half the number of blocks, its third is b minus 1, and its entry k is b plus an offset that depends on k alone, modulo the number of blocks. `live_slots`: the first three entries of each row are 1. `edges_one`: each column has exactly 25 ones. `edges_two`: each column t has exactly 10 ones, all in rows of slots that live_slots marks as used for t's block.
All inputs are finite; a program needn't handle non-finite values.
Results may differ from a plain program's by a relative error of at most 0.00065.
Values may be sent and summed in bfloat16 or wider, within the bound.
A program may use at most 128 MiB of HBM per device.

v0:
```python
import jax
import jax.numpy as jnp
from jax import lax
from jax.sharding import PartitionSpec as P

FAN1 = 25
FAN2 = 10


def from_behind(value, axis, steps):
    count = lax.axis_size(axis)
    pairs = [(source, (source + steps) % count) for source in range(count)]
    return lax.ppermute(value, axis, pairs)


def contract(weight, values):
    return lax.dot_general(
        weight, values, (((0,), (0,)), ((), ())), preferred_element_type=jnp.float32
    )


def contract_exact(weight, values):
    return lax.dot_general(
        weight,
        values,
        (((0,), (0,)), ((), ())),
        precision=lax.Precision.HIGHEST,
        preferred_element_type=jnp.float32,
    )


def fetch_offset(hidden, offset):
    nodes = lax.axis_size("node")
    levels = nodes.bit_length() - 1
    carried = hidden
    for level_bit in range(levels):
        moved = from_behind(carried, "node", nodes - (1 << level_bit))
        carried = jnp.where(offset // (1 << level_bit) % 2 == 1, moved, carried)
    return carried


def local(
    features,
    edges_one,
    w1_self,
    w1_nbr,
    need_blocks,
    live_slots,
    edges_two,
    w2_self,
    w2_nbr,
    labels,
):
    block_len = features.shape[1]
    classes = w2_self.shape[1]
    adjacency = edges_one.astype(jnp.bfloat16)
    neighbour = (jnp.dot(features, adjacency, preferred_element_type=jnp.float32) / FAN1).astype(
        jnp.bfloat16
    )
    before = lax.psum_scatter(
        contract(w1_self, features) + contract(w1_nbr, neighbour),
        "feat",
        scatter_dimension=0,
        tiled=True,
    )
    hidden = jax.nn.relu(before).astype(jnp.bfloat16)
    need_row = need_blocks[0]
    live_row = live_slots[0]
    self_term = contract(w2_self, hidden)
    nodes = lax.axis_size("node")
    mine_index = lax.axis_index("node")
    first_rows = edges_two[0:block_len].astype(jnp.bfloat16)
    gathered = jnp.dot(hidden, first_rows, preferred_element_type=jnp.float32)
    for slot in range(1, need_row.shape[0]):
        offset = (need_row[slot] - mine_index + nodes) % nodes
        sources = fetch_offset(hidden, offset)
        rows = edges_two[slot * block_len : (slot + 1) * block_len].astype(jnp.bfloat16)
        term = jnp.dot(sources, rows, preferred_element_type=jnp.float32)
        gathered = gathered + jnp.where(live_row[slot] == 1, term, 0.0)
    neighbour_term = contract_exact(w2_nbr.astype(jnp.float32), gathered)
    logits = lax.psum(self_term + neighbour_term / FAN2, "feat")
    class_ids = jnp.arange(classes, dtype=jnp.int32)[:, None]
    picked = jnp.sum(jnp.where(class_ids == labels[None, :], logits, 0.0), 0)
    node_loss = jnp.log(jnp.sum(jnp.exp(logits), 0)) - picked
    summed = lax.psum(jnp.sum(node_loss), "node")
    mean_loss = summed / (block_len * lax.axis_size("node"))
    return (node_loss, mean_loss)


def solution(mesh):
    return jax.shard_map(
        local,
        mesh=mesh,
        in_specs=(
            P("feat", "node"),
            P(None, "node"),
            P("feat", None),
            P("feat", None),
            P("node", None),
            P("node", None),
            P(None, "node"),
            P("feat", None),
            P("feat", None),
            P("node"),
        ),
        out_specs=(P("node"), P()),
        check_vma=False,
    )
```

profile of v0, /device:TPU:0, one launch (start us, length us, event | category | flops | bytes accessed | tf_op | source)
XLA Modules:
  0.0 156.6 jit_solution(11803071579191022002)
XLA Ops:
  7.2 0.0 copy-start
  7.2 0.0 copy-start.4
  7.2 0.0 reduce-scatter.2.cloned.1.call-start
  7.2 0.8 copy-done
  8.0 1.0 fusion.49
  9.0 3.8 %fusion.10 = f32[256,1024]{1,0:T(8,128)} fusion(f32[256,1024]{1,0:T(8,128)S(1)} %fusion.49, bf16[25,256]{1,0:T(8,128)(2,1)} %param.13, bf16[25,1024]{1,0:T(8,128)(2,1)S(1)} %copy-done, s32[1024,1024]{1,0:T(8,128)} %param.11), kind=kOutput, calls=%fused_computation.11 | convolution fusion | flops 66897920 | bytes 6355456 | tf_op jit(solution)/shard_map/dot_general | solution.py:17
  12.9 0.0 reduce-scatter.2.cloned.1.call-update
  12.9 0.0 all-reduce.2.cloned.1.call-start
  13.0 27.6 %reduce-scatter.2.cloned.1.call-done = f32[64,1024]{1,0:T(8,128)} async-done(((f32[256,1024]{1,0:T(8,128)}), f32[64,1024]{1,0:T(8,128)}) %reduce-scatter.2.cloned.1.call-update) | async-done | bytes 262160 | tf_op jit(solution)/shard_map/reduce_scatter | solution.py:60
  40.6 1.0 maximum_convert_fusion
  41.5 4.3 %collective-permute-start = (bf16[64,1024]{1,0:T(8,128)(2,1)S(1)}, bf16[64,1024]{1,0:T(8,128)(2,1)S(1)}, u32[]{:S(2)}, u32[]{:S(2)}) collective-permute-start(bf16[64,1024]{1,0:T(8,128)(2,1)S(1)} %maximum_convert_fusion), channel_id=1, source_target_pairs={{0,28},{4,0},{8,4},{12,8},{16,12},{20,16},{24,20},{28,24},{1,29},{... | collective-permute-start | bytes 393224 | tf_op jit(solution)/shard_map/ppermute | solution.py:13
  45.8 0.0 copy-done.4
  45.8 0.6 fusion.48
  48.5 0.0 copy-start.5
  48.6 0.0 copy-start.1
  48.6 9.7 %convert.6 = bf16[4096,1024]{1,0:T(8,128)(2,1)} convert(s32[4096,1024]{1,0:T(8,128)} %param.16) | non-fusion elementwise | flops 4194304 | bytes 25165824 | tf_op jit(solution)/shard_map/convert.3
  58.2 0.0 copy-done.5
  58.3 0.6 fusion.47
  60.7 0.0 collective-permute-done
  60.7 0.0 copy-done.1
  60.8 0.6 collective-permute-start.1
  61.4 2.1 %fusion.6 = f32[64,1024]{1,0:T(8,128)S(1)} fusion(bf16[64,1024]{1,0:T(8,128)(2,1)S(1)} %maximum_convert_fusion, bf16[4096,1024]{1,0:T(8,128)(2,1)} %convert.6), kind=kOutput, calls=%fused_computation.6 | convolution fusion | flops 134217728 | bytes 2490368 | tf_op jit(solution)/shard_map/dot_general | solution.py:73
  63.4 0.6 collective-permute-start.3
  64.0 0.5 collective-permute-start.5
  64.5 1.8 %collective-permute-done.1 = bf16[64,1024]{1,0:T(8,128)(2,1)S(1)} collective-permute-done((bf16[64,1024]{1,0:T(8,128)(2,1)S(1)}, bf16[64,1024]{1,0:T(8,128)(2,1)S(1)}, u32[]{:S(2)}, u32[]{:S(2)}) %collective-permute-start.1) | collective-permute-done | bytes 131104 | tf_op jit(solution)/shard_map/ppermute | solution.py:13
  66.4 0.6 collective-permute-start.2
  67.1 2.8 %collective-permute-done.3 = bf16[64,1024]{1,0:T(8,128)(2,1)S(1)} collective-permute-done((bf16[64,1024]{1,0:T(8,128)(2,1)S(1)}, bf16[64,1024]{1,0:T(8,128)(2,1)S(1)}, u32[]{:S(2)}, u32[]{:S(2)}) %collective-permute-start.3) | collective-permute-done | bytes 131104 | tf_op jit(solution)/shard_map/ppermute | solution.py:13
  69.9 2.2 %collective-permute-start.4 = (bf16[64,1024]{1,0:T(8,128)(2,1)S(1)}, bf16[64,1024]{1,0:T(8,128)(2,1)S(1)}, u32[]{:S(2)}, u32[]{:S(2)}) collective-permute-start(bf16[64,1024]{1,0:T(8,128)(2,1)S(1)} %broadcast_select_fusion.3), channel_id=1, source_target_pairs={{0,16},{4,20},{8,24},{12,28},{16,0},{20,4},{24,8},{28,12},{1,17},{... | collective-permute-start | bytes 393224 | tf_op jit(solution)/shard_map/ppermute | solution.py:13
  72.0 0.0 collective-permute-done.5
  72.1 6.8 %collective-permute-start.6 = (bf16[64,1024]{1,0:T(8,128)(2,1)S(1)}, bf16[64,1024]{1,0:T(8,128)(2,1)S(1)}, u32[]{:S(2)}, u32[]{:S(2)}) collective-permute-start(bf16[64,1024]{1,0:T(8,128)(2,1)S(1)} %broadcast_select_fusion.1), channel_id=1, source_target_pairs={{0,16},{4,20},{8,24},{12,28},{16,0},{20,4},{24,8},{28,12},{1,17},{... | collective-permute-start | bytes 393224 | tf_op jit(solution)/shard_map/ppermute | solution.py:13
  78.8 8.3 %collective-permute-done.4 = bf16[64,1024]{1,0:T(8,128)(2,1)S(1)} collective-permute-done((bf16[64,1024]{1,0:T(8,128)(2,1)S(1)}, bf16[64,1024]{1,0:T(8,128)(2,1)S(1)}, u32[]{:S(2)}, u32[]{:S(2)}) %collective-permute-start.4) | collective-permute-done | bytes 131104 | tf_op jit(solution)/shard_map/ppermute | solution.py:13
  87.2 0.0 copy-start.2
  87.2 2.1 %fusion.20 = f32[64,1024]{1,0:T(8,128)S(1)} fusion(bf16[4096,1024]{1,0:T(8,128)(2,1)} %convert.6, bf16[64,1024]{1,0:T(8,128)(2,1)S(1)} %collective-permute-done.4, bf16[64,1024]{1,0:T(8,128)(2,1)S(1)} %broadcast_select_fusion.3, pred[]{:T(512)S(6)} %eq.78, pred[]{:T(512)} %bitcast.3), kind=kOutput, calls=%fused_computation.15 | convolution fusion | flops 134348800 | bytes 2621953 | tf_op jit(solution)/shard_map/dot_general | solution.py:78
  89.3 0.0 copy-start.6
  89.3 0.0 collective-permute-done.6
  89.3 2.1 %fusion.23 = f32[64,1024]{1,0:T(8,128)S(1)} fusion(bf16[4096,1024]{1,0:T(8,128)(2,1)} %convert.6, bf16[64,1024]{1,0:T(8,128)(2,1)S(1)} %collective-permute-done.6, bf16[64,1024]{1,0:T(8,128)(2,1)S(1)} %broadcast_select_fusion.1, pred[]{:T(512)S(6)} %eq.83, pred[]{:T(512)} %bitcast.5), kind=kOutput, calls=%fused_computation.16 | convolution fusion | flops 134348800 | bytes 2621953 | tf_op jit(solution)/shard_map/dot_general | solution.py:78
  91.4 0.0 collective-permute-done.2
  91.4 2.1 %fusion.26 = f32[64,1024]{1,0:T(8,128)S(1)} fusion(f32[64,1024]{1,0:T(8,128)S(1)} %fusion.23, f32[64,1024]{1,0:T(8,128)S(1)} %fusion.20, f32[64,1024]{1,0:T(8,128)S(1)} %fusion.6, bf16[4096,1024]{1,0:T(8,128)(2,1)} %convert.6, bf16[64,1024]{1,0:T(8,128)(2,1)S(1)} %collective-permute-done.2, bf16[64,1024]{1,0:T(8,128)(2,1)S(1)} %broadcast_select_fusion.5, ...), kind=kOutput, calls=%fused_computation.17 | convolution fusion | flops 134545408 | bytes 3408385 | tf_op jit(solution)/shard_map/dot_general | solution.py:78
  93.5 0.0 copy-done.2
  93.5 0.3 convolution_multiply_fusion
  93.7 0.0 copy-done.3
  93.8 0.8 fusion.29
  94.6 0.0 all-reduce.2.cloned.1.call-update
  94.6 29.2 %all-reduce.2.cloned.1.call-done = f32[47,1024]{1,0:T(8,128)} async-done(((f32[47,1024]{1,0:T(8,128)}), f32[47,1024]{1,0:T(8,128)}) %all-reduce.2.cloned.1.call-update) | async-done | bytes 192528 | tf_op jit(solution)/shard_map/psum | solution.py:81
  123.9 0.0 copy-done.6
  123.9 1.0 exponential_reduce_fusion
  124.8 1.2 fusion.46
  126.0 22.0 %psum.15 = f32[]{:T(128)} all-reduce(f32[]{:T(128)} %get-tuple-element.4), channel_id=1, replica_groups=mesh['node'=8,'feat'=4] {'node'}, use_global_device_ids=true, to_apply=%region_5.6 | all-reduce | flops 1 | bytes 8 | tf_op jit(solution)/shard_map/psum | solution.py:85
  (5 shorter events, 0.1 us)
Async XLA Ops:
  7.2 0.8 copy-start
  7.2 38.7 %copy-start.4 = (s32[1,4]{1,0:T(1,128)S(1)}, s32[1,4]{1,0:T(1,128)}, u32[]{:S(2)}) copy-start(s32[1,4]{1,0:T(1,128)} %param.14) | copy-start | bytes 52
  7.2 33.4 %reduce-scatter.2.cloned.1.call-start = ((), (), s32[]{:S(2)}) async-start(), calls=%async_computation.1 | async-start | bytes 1310720 | tf_op jit(solution)/shard_map/reduce_scatter | solution.py:60
  12.9 110.9 %all-reduce.2.cloned.1.call-start = ((), (), s32[]{:S(2)}) async-start(), calls=%async_computation.2 | async-start | bytes 393216 | tf_op jit(solution)/shard_map/psum | solution.py:81
  41.5 19.2 %collective-permute-start = (bf16[64,1024]{1,0:T(8,128)(2,1)S(1)}, bf16[64,1024]{1,0:T(8,128)(2,1)S(1)}, u32[]{:S(2)}, u32[]{:S(2)}) collective-permute-start(bf16[64,1024]{1,0:T(8,128)(2,1)S(1)} %maximum_convert_fusion), channel_id=1, source_target_pairs={{0,28},{4,0},{8,4},{12,8},{16,12},{20,16},{24,20},{28,24},{1,29},{... | collective-permute-start | bytes 393224 | tf_op jit(solution)/shard_map/ppermute | solution.py:13
  48.5 9.7 %copy-start.5 = (s32[1,4]{1,0:T(1,128)S(1)}, s32[1,4]{1,0:T(1,128)}, u32[]{:S(2)}) copy-start(s32[1,4]{1,0:T(1,128)} %param.15) | copy-start | bytes 52
  48.6 12.2 %copy-start.1 = (f32[64,1024]{1,0:T(8,128)S(1)}, f32[64,1024]{1,0:T(8,128)}, u32[]{:S(2)}) copy-start(f32[64,1024]{1,0:T(8,128)} %reduce-scatter.2.cloned.1.call-done) | copy-start | bytes 786436
  60.8 5.6 %collective-permute-start.1 = (bf16[64,1024]{1,0:T(8,128)(2,1)S(1)}, bf16[64,1024]{1,0:T(8,128)(2,1)S(1)}, u32[]{:S(2)}, u32[]{:S(2)}) collective-permute-start(bf16[64,1024]{1,0:T(8,128)(2,1)S(1)} %get-tuple-element.6), channel_id=1, source_target_pairs={{0,24},{4,28},{8,0},{12,4},{16,8},{20,12},{24,16},{28,20},{1,25},{... | collective-permute-start | bytes 393224 | tf_op jit(solution)/shard_map/ppermute | solution.py:13
  63.4 6.4 %collective-permute-start.3 = (bf16[64,1024]{1,0:T(8,128)(2,1)S(1)}, bf16[64,1024]{1,0:T(8,128)(2,1)S(1)}, u32[]{:S(2)}, u32[]{:S(2)}) collective-permute-start(bf16[64,1024]{1,0:T(8,128)(2,1)S(1)} %get-tuple-element.8), channel_id=1, source_target_pairs={{0,24},{4,28},{8,0},{12,4},{16,8},{20,12},{24,16},{28,20},{1,25},{... | collective-permute-start | bytes 393224 | tf_op jit(solution)/shard_map/ppermute | solution.py:13
  64.0 8.0 %collective-permute-start.5 = (bf16[64,1024]{1,0:T(8,128)(2,1)S(1)}, bf16[64,1024]{1,0:T(8,128)(2,1)S(1)}, u32[]{:S(2)}, u32[]{:S(2)}) collective-permute-start(bf16[64,1024]{1,0:T(8,128)(2,1)S(1)} %get-tuple-element.7), channel_id=1, source_target_pairs={{0,24},{4,28},{8,0},{12,4},{16,8},{20,12},{24,16},{28,20},{1,25},{... | collective-permute-start | bytes 393224 | tf_op jit(solution)/shard_map/ppermute | solution.py:13
  66.4 25.0 %collective-permute-start.2 = (bf16[64,1024]{1,0:T(8,128)(2,1)S(1)}, bf16[64,1024]{1,0:T(8,128)(2,1)S(1)}, u32[]{:S(2)}, u32[]{:S(2)}) collective-permute-start(bf16[64,1024]{1,0:T(8,128)(2,1)S(1)} %broadcast_select_fusion.5), channel_id=1, source_target_pairs={{0,16},{4,20},{8,24},{12,28},{16,0},{20,4},{24,8},{28,12},{1,17},{... | collective-permute-start | bytes 393224 | tf_op jit(solution)/shard_map/ppermute | solution.py:13
  69.9 17.3 %collective-permute-start.4 = (bf16[64,1024]{1,0:T(8,128)(2,1)S(1)}, bf16[64,1024]{1,0:T(8,128)(2,1)S(1)}, u32[]{:S(2)}, u32[]{:S(2)}) collective-permute-start(bf16[64,1024]{1,0:T(8,128)(2,1)S(1)} %broadcast_select_fusion.3), channel_id=1, source_target_pairs={{0,16},{4,20},{8,24},{12,28},{16,0},{20,4},{24,8},{28,12},{1,17},{... | collective-permute-start | bytes 393224 | tf_op jit(solution)/shard_map/ppermute | solution.py:13
  72.1 17.2 %collective-permute-start.6 = (bf16[64,1024]{1,0:T(8,128)(2,1)S(1)}, bf16[64,1024]{1,0:T(8,128)(2,1)S(1)}, u32[]{:S(2)}, u32[]{:S(2)}) collective-permute-start(bf16[64,1024]{1,0:T(8,128)(2,1)S(1)} %broadcast_select_fusion.1), channel_id=1, source_target_pairs={{0,16},{4,20},{8,24},{12,28},{16,0},{20,4},{24,8},{28,12},{1,17},{... | collective-permute-start | bytes 393224 | tf_op jit(solution)/shard_map/ppermute | solution.py:13
  87.2 6.3 %copy-start.2 = (bf16[64,47]{0,1:T(8,128)(2,1)S(1)}, bf16[64,47]{0,1:T(8,128)(2,1)}, u32[]{:S(2)}) copy-start(bf16[64,47]{0,1:T(8,128)(2,1)} %param.18) | copy-start | bytes 18052
  87.2 6.6 %copy-start.3 = (bf16[64,47]{0,1:T(8,128)(2,1)S(1)}, bf16[64,47]{0,1:T(8,128)(2,1)}, u32[]{:S(2)}) copy-start(bf16[64,47]{0,1:T(8,128)(2,1)} %param.17) | copy-start | bytes 18052
  89.3 34.6 %copy-start.6 = (s32[1024]{0:T(1024)S(1)}, s32[1024]{0:T(1024)}, u32[]{:S(2)}) copy-start(s32[1024]{0:T(1024)} %param.19) | copy-start | bytes 12292
Sparse Core Ops, SparseCore 0:
  13.0 27.4 reduce-scatter.1
  94.7 29.0 all-reduce.1
where the time goes:
time: 157 us
  waiting for transfers between devices  69.8 us (44%)
  blocking collectives  22 us (14%)
  between operations  20 us (13%)
  starting transfers between devices  15.7 us (10%)
  matrix products  14.3 us (9%)
  other arithmetic  12.9 us (8%)
  local copies, waits for them, and re-layouts  1.99 us (1%)
    psum x1, waiting for transfers between devices, local(): logits = lax.psum(self_term + neighbour_term / FAN2, 'feat')  29.2 us
    reduce_scatter x1, waiting for transfers between devices, local(): lax.psum_scatter(contract(w1_self, features) + contract(w1_nbr, neighbour...  27.6 us
    psum x1, blocking collectives, local(): summed = lax.psum(jnp.sum(node_loss), 'node')  22 us
    ppermute x7, starting transfers between devices, from_behind(): return lax.ppermute(value, axis, pairs)  15.6 us
    ppermute x7, waiting for transfers between devices, from_behind(): return lax.ppermute(value, axis, pairs)  13 us
    another operation x1, other arithmetic  9.68 us
    dot_general x3, matrix products, local(): term = jnp.dot(sources, rows, preferred_element_type=jnp.float32)  6.26 us
    dot_general x3, matrix products, contract(): lax.dot_general(weight, values, (((0,), (0,)), ((), ())), preferred_eleme...  5.7 us
  transfers between devices with their start and end apart: 9, of which 5 were waited for; matrix products, arithmetic and copies ran while one was open for 11% of the time, Pallas kernels for 0%

commit v1 on v0

--- a/solution.py
+++ b/solution.py
@@ -78,7 +78,9 @@
         term = jnp.dot(sources, rows, preferred_element_type=jnp.float32)
         gathered = gathered + jnp.where(live_row[slot] == 1, term, 0.0)
     neighbour_term = contract_exact(w2_nbr.astype(jnp.float32), gathered)
-    logits = lax.psum(self_term + neighbour_term / FAN2, "feat")
+    block = self_term + neighbour_term / FAN2
+    parts = lax.all_gather(block, "feat", axis=0, tiled=False)
+    logits = parts.sum(axis=0)
     class_ids = jnp.arange(classes, dtype=jnp.int32)[:, None]
     picked = jnp.sum(jnp.where(class_ids == labels[None, :], logits, 0.0), 0)
     node_loss = jnp.log(jnp.sum(jnp.exp(logits), 0)) - picked

time: 157 us -> 132 us (0.84)
  waiting for transfers between devices: 69.8 us -> 40.6 us
  blocking collectives: 22 us -> 27.4 us
    psum x1 -> x0, waiting for transfers between devices: 29.2 us -> none  [local(): logits = lax.psum(self_term + neighbour_term / FAN2, 'feat')]
    all_gather x0 -> x1, blocking collectives: none -> 7.67 us  [local(): parts = lax.all_gather(block, 'feat', axis=0, tiled=False)]
    psum x1, blocking collectives: 22 us -> 19.8 us  [local(): summed = lax.psum(jnp.sum(node_loss), 'node')]
  transfers between devices with their start and end apart: 9 -> 8, of which waited for: 5 -> 4; matrix products, arithmetic and copies ran while one was open for 11% -> 13% of each run, Pallas kernels for 0% -> 0%
where the time goes in v1:
time: 132 us
  waiting for transfers between devices  40.6 us (31%)
  blocking collectives  27.4 us (21%)
  between operations  20.2 us (15%)
  starting transfers between devices  15.6 us (12%)
  matrix products  13.6 us (10%)
  other arithmetic  12 us (9%)
  local copies, waits for them, and re-layouts  2.06 us (2%)
    reduce_scatter x1, waiting for transfers between devices, local(): lax.psum_scatter(contract(w1_self, features) + contract(w1_nbr, neighbour...  27.7 us
    psum x1, blocking collectives, local(): summed = lax.psum(jnp.sum(node_loss), 'node')  19.8 us
    ppermute x7, starting transfers between devices, from_behind(): return lax.ppermute(value, axis, pairs)  15.6 us
    ppermute x7, waiting for transfers between devices, from_behind(): return lax.ppermute(value, axis, pairs)  13 us
    another operation x1, other arithmetic  9.66 us
    all_gather x1, blocking collectives, local(): parts = lax.all_gather(block, 'feat', axis=0, tiled=False)  7.67 us
    dot_general x3, matrix products, local(): term = jnp.dot(sources, rows, preferred_element_type=jnp.float32)  6.26 us
    dot_general x3, matrix products, contract(): lax.dot_general(weight, values, (((0,), (0,)), ((), ())), preferred_eleme...  5.03 us
  transfers between devices with their start and end apart: 8, of which 4 were waited for; matrix products, arithmetic and copies ran while one was open for 13% of the time, Pallas kernels for 0%

profile of v1, /device:TPU:0, one launch (start us, length us, event | category | flops | bytes accessed | tf_op | source)
XLA Modules:
  0.0 131.5 jit_solution(10531280238830266225)
XLA Ops:
  7.2 0.0 copy-start
  7.2 0.0 copy-start.4
  7.2 0.0 reduce-scatter.2.cloned.1.call-start
  7.2 0.8 copy-done
  8.0 1.0 fusion.49
  9.0 3.8 %fusion.10 = f32[256,1024]{1,0:T(8,128)} fusion(f32[256,1024]{1,0:T(8,128)S(1)} %fusion.49, bf16[25,256]{1,0:T(8,128)(2,1)} %param.13, bf16[25,1024]{1,0:T(8,128)(2,1)S(1)} %copy-done, s32[1024,1024]{1,0:T(8,128)} %param.11), kind=kOutput, calls=%fused_computation.11 | convolution fusion | flops 66897920 | bytes 6355456 | tf_op jit(solution)/shard_map/dot_general | solution.py:17
  12.9 0.0 reduce-scatter.2.cloned.1.call-update
  12.9 27.7 %reduce-scatter.2.cloned.1.call-done = f32[64,1024]{1,0:T(8,128)} async-done(((f32[256,1024]{1,0:T(8,128)}), f32[64,1024]{1,0:T(8,128)}) %reduce-scatter.2.cloned.1.call-update) | async-done | bytes 262160 | tf_op jit(solution)/shard_map/reduce_scatter | solution.py:60
  40.6 1.0 maximum_convert_fusion
  41.5 4.3 %collective-permute-start = (bf16[64,1024]{1,0:T(8,128)(2,1)S(1)}, bf16[64,1024]{1,0:T(8,128)(2,1)S(1)}, u32[]{:S(2)}, u32[]{:S(2)}) collective-permute-start(bf16[64,1024]{1,0:T(8,128)(2,1)S(1)} %maximum_convert_fusion), channel_id=1, source_target_pairs={{0,28},{4,0},{8,4},{12,8},{16,12},{20,16},{24,20},{28,24},{1,29},{... | collective-permute-start | bytes 393224 | tf_op jit(solution)/shard_map/ppermute | solution.py:13
  45.8 0.0 copy-done.4
  45.8 0.6 fusion.48
  48.6 0.0 copy-start.5
  48.6 0.0 copy-start.1
  48.6 9.7 %convert.6 = bf16[4096,1024]{1,0:T(8,128)(2,1)} convert(s32[4096,1024]{1,0:T(8,128)} %param.16) | non-fusion elementwise | flops 4194304 | bytes 25165824 | tf_op jit(solution)/shard_map/convert.3
  58.3 0.0 copy-done.5
  58.3 0.7 fusion.47
  60.9 0.0 collective-permute-done
  60.9 0.0 copy-done.1
  61.0 0.6 collective-permute-start.1
  61.6 2.1 %fusion.6 = f32[64,1024]{1,0:T(8,128)S(1)} fusion(bf16[64,1024]{1,0:T(8,128)(2,1)S(1)} %maximum_convert_fusion, bf16[4096,1024]{1,0:T(8,128)(2,1)} %convert.6), kind=kOutput, calls=%fused_computation.6 | convolution fusion | flops 134217728 | bytes 2490368 | tf_op jit(solution)/shard_map/dot_general | solution.py:73
  63.6 0.6 collective-permute-start.3
  64.2 0.5 collective-permute-start.5
  64.8 1.8 %collective-permute-done.1 = bf16[64,1024]{1,0:T(8,128)(2,1)S(1)} collective-permute-done((bf16[64,1024]{1,0:T(8,128)(2,1)S(1)}, bf16[64,1024]{1,0:T(8,128)(2,1)S(1)}, u32[]{:S(2)}, u32[]{:S(2)}) %collective-permute-start.1) | collective-permute-done | bytes 131104 | tf_op jit(solution)/shard_map/ppermute | solution.py:13
  66.6 0.6 collective-permute-start.2
  67.3 2.8 %collective-permute-done.3 = bf16[64,1024]{1,0:T(8,128)(2,1)S(1)} collective-permute-done((bf16[64,1024]{1,0:T(8,128)(2,1)S(1)}, bf16[64,1024]{1,0:T(8,128)(2,1)S(1)}, u32[]{:S(2)}, u32[]{:S(2)}) %collective-permute-start.3) | collective-permute-done | bytes 131104 | tf_op jit(solution)/shard_map/ppermute | solution.py:13
  70.1 2.2 %collective-permute-start.4 = (bf16[64,1024]{1,0:T(8,128)(2,1)S(1)}, bf16[64,1024]{1,0:T(8,128)(2,1)S(1)}, u32[]{:S(2)}, u32[]{:S(2)}) collective-permute-start(bf16[64,1024]{1,0:T(8,128)(2,1)S(1)} %broadcast_select_fusion.3), channel_id=1, source_target_pairs={{0,16},{4,20},{8,24},{12,28},{16,0},{20,4},{24,8},{28,12},{1,17},{... | collective-permute-start | bytes 393224 | tf_op jit(solution)/shard_map/ppermute | solution.py:13
  72.3 0.0 collective-permute-done.5
  72.3 6.8 %collective-permute-start.6 = (bf16[64,1024]{1,0:T(8,128)(2,1)S(1)}, bf16[64,1024]{1,0:T(8,128)(2,1)S(1)}, u32[]{:S(2)}, u32[]{:S(2)}) collective-permute-start(bf16[64,1024]{1,0:T(8,128)(2,1)S(1)} %broadcast_select_fusion.1), channel_id=1, source_target_pairs={{0,16},{4,20},{8,24},{12,28},{16,0},{20,4},{24,8},{28,12},{1,17},{... | collective-permute-start | bytes 393224 | tf_op jit(solution)/shard_map/ppermute | solution.py:13
  79.0 8.3 %collective-permute-done.4 = bf16[64,1024]{1,0:T(8,128)(2,1)S(1)} collective-permute-done((bf16[64,1024]{1,0:T(8,128)(2,1)S(1)}, bf16[64,1024]{1,0:T(8,128)(2,1)S(1)}, u32[]{:S(2)}, u32[]{:S(2)}) %collective-permute-start.4) | collective-permute-done | bytes 131104 | tf_op jit(solution)/shard_map/ppermute | solution.py:13
  87.4 0.0 copy-start.2
  87.4 0.0 copy-start.3
  87.4 2.1 %fusion.20 = f32[64,1024]{1,0:T(8,128)S(1)} fusion(bf16[4096,1024]{1,0:T(8,128)(2,1)} %convert.6, bf16[64,1024]{1,0:T(8,128)(2,1)S(1)} %collective-permute-done.4, bf16[64,1024]{1,0:T(8,128)(2,1)S(1)} %broadcast_select_fusion.3, pred[]{:T(512)S(6)} %eq.78, pred[]{:T(512)} %bitcast.3), kind=kOutput, calls=%fused_computation.15 | convolution fusion | flops 134348800 | bytes 2621953 | tf_op jit(solution)/shard_map/dot_general | solution.py:78
  89.5 0.0 collective-permute-done.6
  89.5 0.0 copy-start.6
  89.5 2.1 %fusion.23 = f32[64,1024]{1,0:T(8,128)S(1)} fusion(bf16[4096,1024]{1,0:T(8,128)(2,1)} %convert.6, bf16[64,1024]{1,0:T(8,128)(2,1)S(1)} %collective-permute-done.6, bf16[64,1024]{1,0:T(8,128)(2,1)S(1)} %broadcast_select_fusion.1, pred[]{:T(512)S(6)} %eq.83, pred[]{:T(512)} %bitcast.5), kind=kOutput, calls=%fused_computation.16 | convolution fusion | flops 134348800 | bytes 2621953 | tf_op jit(solution)/shard_map/dot_general | solution.py:78
  91.6 0.0 collective-permute-done.2
  91.6 2.1 %fusion.26 = f32[64,1024]{1,0:T(8,128)S(1)} fusion(f32[64,1024]{1,0:T(8,128)S(1)} %fusion.23, f32[64,1024]{1,0:T(8,128)S(1)} %fusion.20, f32[64,1024]{1,0:T(8,128)S(1)} %fusion.6, bf16[4096,1024]{1,0:T(8,128)(2,1)} %convert.6, bf16[64,1024]{1,0:T(8,128)(2,1)S(1)} %collective-permute-done.2, bf16[64,1024]{1,0:T(8,128)(2,1)S(1)} %broadcast_select_fusion.5, ...), kind=kOutput, calls=%fused_computation.17 | convolution fusion | flops 134545408 | bytes 3408385 | tf_op jit(solution)/shard_map/dot_general | solution.py:78
  93.7 0.0 copy-done.2
  93.7 0.3 convolution_multiply_fusion
  94.0 0.0 copy-done.3
  94.0 0.2 fusion.29
  94.1 7.7 %all-gather.1 = f32[4,47,1024]{2,1,0:T(8,128)S(1)} all-gather(f32[1,47,1024]{2,1,0:T(8,128)S(1)} %fusion.29), channel_id=2, replica_groups=mesh['node'=8,'feat'=4] {'feat'}, dimensions={0}, use_global_device_ids=true | all-gather | bytes 962560 | tf_op jit(solution)/shard_map/all_gather | solution.py:82
  101.9 0.0 copy-done.6
  101.9 0.1 exponential_reduce_fusion
  101.9 1.2 fusion.46
  103.1 19.8 %psum.7 = f32[]{:T(128)} all-reduce(f32[]{:T(128)} %get-tuple-element.4), channel_id=1, replica_groups=mesh['node'=8,'feat'=4] {'node'}, use_global_device_ids=true, to_apply=%region_5.6 | all-reduce | flops 1 | bytes 8 | tf_op jit(solution)/shard_map/psum | solution.py:87
  (5 shorter events, 0.1 us)
Async XLA Ops:
  7.2 0.8 copy-start
  7.2 38.7 %copy-start.4 = (s32[1,4]{1,0:T(1,128)S(1)}, s32[1,4]{1,0:T(1,128)}, u32[]{:S(2)}) copy-start(s32[1,4]{1,0:T(1,128)} %param.14) | copy-start | bytes 52
  7.2 33.4 %reduce-scatter.2.cloned.1.call-start = ((), (), s32[]{:S(2)}) async-start(), calls=%async_computation.1 | async-start | bytes 1310720 | tf_op jit(solution)/shard_map/reduce_scatter | solution.py:60
  41.5 19.4 %collective-permute-start = (bf16[64,1024]{1,0:T(8,128)(2,1)S(1)}, bf16[64,1024]{1,0:T(8,128)(2,1)S(1)}, u32[]{:S(2)}, u32[]{:S(2)}) collective-permute-start(bf16[64,1024]{1,0:T(8,128)(2,1)S(1)} %maximum_convert_fusion), channel_id=1, source_target_pairs={{0,28},{4,0},{8,4},{12,8},{16,12},{20,16},{24,20},{28,24},{1,29},{... | collective-permute-start | bytes 393224 | tf_op jit(solution)/shard_map/ppermute | solution.py:13
  48.6 9.7 %copy-start.5 = (s32[1,4]{1,0:T(1,128)S(1)}, s32[1,4]{1,0:T(1,128)}, u32[]{:S(2)}) copy-start(s32[1,4]{1,0:T(1,128)} %param.15) | copy-start | bytes 52
  48.6 12.3 %copy-start.1 = (f32[64,1024]{1,0:T(8,128)S(1)}, f32[64,1024]{1,0:T(8,128)}, u32[]{:S(2)}) copy-start(f32[64,1024]{1,0:T(8,128)} %reduce-scatter.2.cloned.1.call-done) | copy-start | bytes 786436
  61.0 5.6 %collective-permute-start.1 = (bf16[64,1024]{1,0:T(8,128)(2,1)S(1)}, bf16[64,1024]{1,0:T(8,128)(2,1)S(1)}, u32[]{:S(2)}, u32[]{:S(2)}) collective-permute-start(bf16[64,1024]{1,0:T(8,128)(2,1)S(1)} %get-tuple-element.6), channel_id=1, source_target_pairs={{0,24},{4,28},{8,0},{12,4},{16,8},{20,12},{24,16},{28,20},{1,25},{... | collective-permute-start | bytes 393224 | tf_op jit(solution)/shard_map/ppermute | solution.py:13
  63.6 6.4 %collective-permute-start.3 = (bf16[64,1024]{1,0:T(8,128)(2,1)S(1)}, bf16[64,1024]{1,0:T(8,128)(2,1)S(1)}, u32[]{:S(2)}, u32[]{:S(2)}) collective-permute-start(bf16[64,1024]{1,0:T(8,128)(2,1)S(1)} %get-tuple-element.8), channel_id=1, source_target_pairs={{0,24},{4,28},{8,0},{12,4},{16,8},{20,12},{24,16},{28,20},{1,25},{... | collective-permute-start | bytes 393224 | tf_op jit(solution)/shard_map/ppermute | solution.py:13
  64.2 8.0 %collective-permute-start.5 = (bf16[64,1024]{1,0:T(8,128)(2,1)S(1)}, bf16[64,1024]{1,0:T(8,128)(2,1)S(1)}, u32[]{:S(2)}, u32[]{:S(2)}) collective-permute-start(bf16[64,1024]{1,0:T(8,128)(2,1)S(1)} %get-tuple-element.7), channel_id=1, source_target_pairs={{0,24},{4,28},{8,0},{12,4},{16,8},{20,12},{24,16},{28,20},{1,25},{... | collective-permute-start | bytes 393224 | tf_op jit(solution)/shard_map/ppermute | solution.py:13
  66.6 25.0 %collective-permute-start.2 = (bf16[64,1024]{1,0:T(8,128)(2,1)S(1)}, bf16[64,1024]{1,0:T(8,128)(2,1)S(1)}, u32[]{:S(2)}, u32[]{:S(2)}) collective-permute-start(bf16[64,1024]{1,0:T(8,128)(2,1)S(1)} %broadcast_select_fusion.5), channel_id=1, source_target_pairs={{0,16},{4,20},{8,24},{12,28},{16,0},{20,4},{24,8},{28,12},{1,17},{... | collective-permute-start | bytes 393224 | tf_op jit(solution)/shard_map/ppermute | solution.py:13
  70.1 17.3 %collective-permute-start.4 = (bf16[64,1024]{1,0:T(8,128)(2,1)S(1)}, bf16[64,1024]{1,0:T(8,128)(2,1)S(1)}, u32[]{:S(2)}, u32[]{:S(2)}) collective-permute-start(bf16[64,1024]{1,0:T(8,128)(2,1)S(1)} %broadcast_select_fusion.3), channel_id=1, source_target_pairs={{0,16},{4,20},{8,24},{12,28},{16,0},{20,4},{24,8},{28,12},{1,17},{... | collective-permute-start | bytes 393224 | tf_op jit(solution)/shard_map/ppermute | solution.py:13
  72.3 17.2 %collective-permute-start.6 = (bf16[64,1024]{1,0:T(8,128)(2,1)S(1)}, bf16[64,1024]{1,0:T(8,128)(2,1)S(1)}, u32[]{:S(2)}, u32[]{:S(2)}) collective-permute-start(bf16[64,1024]{1,0:T(8,128)(2,1)S(1)} %broadcast_select_fusion.1), channel_id=1, source_target_pairs={{0,16},{4,20},{8,24},{12,28},{16,0},{20,4},{24,8},{28,12},{1,17},{... | collective-permute-start | bytes 393224 | tf_op jit(solution)/shard_map/ppermute | solution.py:13
  87.4 6.3 %copy-start.2 = (bf16[64,47]{0,1:T(8,128)(2,1)S(1)}, bf16[64,47]{0,1:T(8,128)(2,1)}, u32[]{:S(2)}) copy-start(bf16[64,47]{0,1:T(8,128)(2,1)} %param.18) | copy-start | bytes 18052
  87.4 6.6 %copy-start.3 = (bf16[64,47]{0,1:T(8,128)(2,1)S(1)}, bf16[64,47]{0,1:T(8,128)(2,1)}, u32[]{:S(2)}) copy-start(bf16[64,47]{0,1:T(8,128)(2,1)} %param.17) | copy-start | bytes 18052
  89.5 12.4 %copy-start.6 = (s32[1024]{0:T(1024)S(1)}, s32[1024]{0:T(1024)}, u32[]{:S(2)}) copy-start(s32[1024]{0:T(1024)} %param.19) | copy-start | bytes 12292
Sparse Core Ops, SparseCore 0:
  13.0 27.4 reduce-scatter.1
